TPU v7x, 32 devices: a whole 2x2x4 slice. The times are simulated.
32 devices in a mesh: ep: 16 (over z, y, x), dp: 2 (over core).
Axes of the slice: x: 2, y: 2, z: 4, core: 2. Of those that a mesh axis runs over, the one named last changes fastest.
Arguments:
- layer_input: bfloat16 [2048, 3584], P('ep'), may hold values from -6 to 6
- out_grad: bfloat16 [2048, 3584], P('ep'), may hold values from -6 to 6
- expert_ids: int32 [2048, 8], P('ep'), may hold values from 0 to 15, all different within a row; in each aligned block of 128 rows (0 to 127, 128 to 255, ...) at most 80 rows name the same one
- gate_probs: float32 [2048, 8], P('ep'), may hold values from 0.1 to 1
- gate_proj: bfloat16 [16, 3584, 1024], P('ep'), may hold values from -0.09375 to 0.09375
- up_proj: bfloat16 [16, 3584, 1024], P('ep'), may hold values from -0.09375 to 0.09375
- down_proj: bfloat16 [16, 1024, 3584], P('ep'), may hold values from -0.1875 to 0.1875
Outputs:
- input_grad: bfloat16 [2048, 3584], P('ep', 'dp')
Inputs may be any that keep to these rules, and one draw needn't show every extreme that they name: `expert_ids`: each row names 8 different experts. The 128 rows of one device name one expert at most 80 times, and in every draw some device's rows name some expert exactly 80 times.
All inputs are finite; a program needn't handle non-finite values.
Results may differ from a plain program's by a relative error of at most 0.0058.
Values may be sent and summed in bfloat16 or wider, within the bound.
A program may use at most 192 MiB of HBM per device.

v0:
```python
import jax
import jax.numpy as jnp
from jax import lax
from jax.sharding import PartitionSpec as P


def body(layer_input, out_grad, expert_ids, gate_probs, gate_proj, up_proj, down_proj):
    experts = lax.axis_size("ep")
    halves = lax.axis_size("dp")
    tok_rows, features = layer_input.shape
    half = tok_rows // halves
    core = lax.axis_index("dp")
    start = core * half
    mine_in = lax.dynamic_slice_in_dim(layer_input, start, half, 0)
    mine_grad = lax.dynamic_slice_in_dim(out_grad, start, half, 0)
    ids = lax.dynamic_slice_in_dim(expert_ids, start, half, 0)
    probs = lax.dynamic_slice_in_dim(gate_probs, start, half, 0)
    names = jnp.arange(experts, dtype=jnp.int32)
    table = jnp.sum(
        jnp.where(ids[None, :, :] == names[:, None, None], probs[None, :, :], 0.0), axis=2
    )
    weight = lax.all_to_all(table, "ep", split_axis=0, concat_axis=0, tiled=True).reshape(-1)
    in_rows = lax.all_gather(mine_in, "ep", axis=0, tiled=True)
    grad_rows = lax.all_gather(mine_grad, "ep", axis=0, tiled=True)
    gate_mat, up_mat, down_mat = (gate_proj[0], up_proj[0], down_proj[0])
    nt = (((1,), (1,)), ((), ()))
    gate_pre = jnp.dot(in_rows, gate_mat, preferred_element_type=jnp.float32)
    up_pre = jnp.dot(in_rows, up_mat, preferred_element_type=jnp.float32)
    hidden_grad = lax.dot_general(grad_rows, down_mat, nt, preferred_element_type=jnp.float32)
    s = jax.nn.sigmoid(gate_pre)
    gate_grad = (hidden_grad * up_pre * s * (1.0 + gate_pre * (1.0 - s))).astype(jnp.bfloat16)
    up_grad = (hidden_grad * gate_pre * s).astype(jnp.bfloat16)
    back = lax.dot_general(gate_grad, gate_mat, nt, preferred_element_type=jnp.float32)
    back = back + lax.dot_general(up_grad, up_mat, nt, preferred_element_type=jnp.float32)
    back = (back * weight[:, None]).astype(jnp.bfloat16)
    mine = lax.psum_scatter(back, "ep", scatter_dimension=0, tiled=True)
    return lax.all_to_all(mine, "dp", split_axis=1, concat_axis=0, tiled=True)


def solution(mesh):
    row = P("ep", None)
    mat = P("ep", None, None)
    return jax.shard_map(
        body,
        mesh=mesh,
        in_specs=(row, row, row, row, mat, mat, mat),
        out_specs=P("ep", "dp"),
        check_vma=False,
    )
```

profile of v0, /device:TPU:11, one launch (start us, length us, event | category | flops | bytes accessed | tf_op | source)
XLA Modules:
  0.0 442.3 jit_solution(1134362332234248369)
XLA Ops:
  6.5 0.0 copy-start
  6.5 0.0 all-gather.3.cloned.1.call-start
  6.5 1.2 copy-done
  7.7 0.8 constant_dynamic-slice_fusion.3
  8.5 0.0 all-gather.3.cloned.1.call-update
  8.6 0.0 all-gather.5.cloned.1.call-start
  8.6 1.8 constant_dynamic-slice_fusion.2
  10.4 0.0 all-gather.5.cloned.1.call-update
  10.5 0.0 reduce-scatter.2.cloned.1.call-start
  10.5 0.8 constant_dynamic-slice_fusion.1
  11.3 0.8 constant_dynamic-slice_fusion
  12.1 10.6 %all_to_all.28 = f32[16,1,64]{2,1,0:T(1,128)S(1)} all-to-all(f32[16,1,64]{2,1,0:T(1,128)S(1)} %bitcast.32), channel_id=1, replica_groups=mesh['ep'=16,'dp'=2] {'ep'}, dimensions={0} | all-to-all | bytes 8192 | tf_op jit(solution)/shard_map/all_to_all | solution.py:22
  22.7 0.6 broadcast.14
  23.2 0.7 reduce.3
  23.9 0.1 mul.38
  24.0 87.5 %all-gather.3.cloned.1.call-done = bf16[1024,3584]{1,0:T(8,128)(2,1)} async-done(((bf16[64,3584]{1,0:T(8,128)(2,1)}), bf16[1024,3584]{1,0:T(8,128)(2,1)}) %all-gather.3.cloned.1.call-update) | async-done | bytes 7340048 | tf_op jit(solution)/shard_map/all_gather | solution.py:24
  111.5 13.6 %fusion.7 = f32[1024,1024]{1,0:T(8,128)} fusion(bf16[1024,3584]{1,0:T(8,128)(2,1)} %all-gather.3.cloned.1.call-done, bf16[1,1024,3584]{2,1,0:T(8,128)(2,1)} %param.13), kind=kOutput, calls=%fused_computation.8 | convolution fusion | flops 7516192768 | bytes 18874368 | tf_op jit(solution)/shard_map/dot_general | solution.py:29
  125.1 90.3 %all-gather.5.cloned.1.call-done = bf16[1024,3584]{1,0:T(8,128)(2,1)} async-done(((bf16[64,3584]{1,0:T(8,128)(2,1)}), bf16[1024,3584]{1,0:T(8,128)(2,1)}) %all-gather.5.cloned.1.call-update) | async-done | bytes 7340048 | tf_op jit(solution)/shard_map/all_gather | solution.py:23
  215.4 0.0 copy-start.2
  215.4 0.0 copy-start.3
  215.4 0.0 slice-start
  215.4 13.6 %fusion.2 = f32[1024,1024]{1,0:T(8,128)} fusion(bf16[1024,3584]{1,0:T(8,128)(2,1)} %all-gather.5.cloned.1.call-done, bf16[1,3584,1024]{2,1,0:T(8,128)(2,1)} %param.11), kind=kOutput, calls=%fused_computation.3 | convolution fusion | flops 7516192768 | bytes 18874368 | tf_op jit(solution)/shard_map/dot_general | solution.py:27
  229.0 0.0 copy-done.2
  229.0 0.0 copy-done.3
  229.0 0.0 slice-start.1
  229.0 11.8 %multiply_convert_fusion.2 = bf16[1024,1024]{1,0:T(8,128)(2,1)S(1)} fusion(f32[1024,1024]{1,0:T(8,128)} %fusion.2, f32[1024,1024]{1,0:T(8,128)S(1)} %copy-done.3, bf16[1024,3584]{1,0:T(8,128)(2,1)S(1)} %copy-done.2, bf16[1,3584,1024]{2,1,0:T(8,128)(2,1)} %param.12), kind=kOutput, calls=%fused_computation.11 | convolution fusion | flops 7526678528 | bytes 25165824 | tf_op jit(solution)/shard_map/dot_general | solution.py:28
  240.9 0.0 slice-done
  240.9 0.0 slice-done.1
  240.9 10.7 %fusion = f32[1024,3584]{1,0:T(8,128)} fusion(bf16[1024,1024]{1,0:T(8,128)(2,1)S(1)} %multiply_convert_fusion.2, bf16[1,3584,1024]{2,1,0:T(8,128)(2,1)S(1)} %bitcast.34), kind=kOutput, calls=%fused_computation.1 | convolution fusion | flops 7516192768 | bytes 24117248 | tf_op jit(solution)/shard_map/dot_general | solution.py:33
  251.6 0.0 copy-start.1
  251.6 17.7 %multiply_convert_fusion = bf16[1024,3584]{1,0:T(8,128)(2,1)} fusion(f32[1024,3584]{1,0:T(8,128)} %fusion, bf16[1,3584,1024]{2,1,0:T(8,128)(2,1)} %param.12, f32[1024]{0:T(1024)S(1)} %mul.38, f32[1024,1024]{1,0:T(8,128)} %fusion.7, f32[1024,1024]{1,0:T(8,128)} %fusion.2), kind=kOutput, calls=%fused_computation | convolution fusion | flops 7533494272 | bytes 37752832 | tf_op jit(solution)/shard_map/dot_general | solution.py:34
  269.3 0.0 reduce-scatter.2.cloned.1.call-update
  269.4 159.9 %reduce-scatter.2.cloned.1.call-done = bf16[64,3584]{1,0:T(8,128)(2,1)} async-done(((bf16[1024,3584]{1,0:T(8,128)(2,1)}), bf16[64,3584]{1,0:T(8,128)(2,1)}) %reduce-scatter.2.cloned.1.call-update) | async-done | bytes 458768 | tf_op jit(solution)/shard_map/reduce_scatter | solution.py:36
  429.2 1.0 copy.18
  430.3 4.7 %all_to_all.29 = bf16[64,2,1792]{2,0,1:T(8,128)(2,1)S(1)} all-to-all(bf16[64,2,1792]{2,0,1:T(8,128)(2,1)S(1)} %bitcast.29), channel_id=1, replica_groups=mesh['ep'=16,'dp'=2] {'dp'}, dimensions={1} | all-to-all | bytes 917504 | tf_op jit(solution)/shard_map/all_to_all | solution.py:37
  435.0 0.8 copy.20
  435.7 0.0 copy-done.1
  (2 shorter events, 0.0 us)
Async XLA Ops:
  6.5 1.2 copy-start
  6.5 105.0 %all-gather.3.cloned.1.call-start = ((), (), s32[]{:S(2)}) async-start(), calls=%async_computation.3 | async-start | bytes 7798784 | tf_op jit(solution)/shard_map/all_gather | solution.py:24
  8.6 206.9 %all-gather.5.cloned.1.call-start = ((), (), s32[]{:S(2)}) async-start(), calls=%async_computation.4 | async-start | bytes 7798784 | tf_op jit(solution)/shard_map/all_gather | solution.py:23
  10.5 418.8 %reduce-scatter.2.cloned.1.call-start = ((), (), s32[]{:S(2)}) async-start(), calls=%async_computation.5 | async-start | bytes 7798784 | tf_op jit(solution)/shard_map/reduce_scatter | solution.py:36
  215.4 13.6 %copy-start.2 = (bf16[1024,3584]{1,0:T(8,128)(2,1)S(1)}, bf16[1024,3584]{1,0:T(8,128)(2,1)}, u32[]{:S(2)}) copy-start(bf16[1024,3584]{1,0:T(8,128)(2,1)} %all-gather.5.cloned.1.call-done) | copy-start | bytes 22020100
  215.4 13.6 %copy-start.3 = (f32[1024,1024]{1,0:T(8,128)S(1)}, f32[1024,1024]{1,0:T(8,128)}, u32[]{:S(2)}) copy-start(f32[1024,1024]{1,0:T(8,128)} %fusion.7) | copy-start | bytes 12582916
  215.4 25.5 %slice-start = ((s8[7340032]{0:T(1024)(128)(4,1)}), s8[4194304]{0:T(1024)(128)(4,1)S(1)}, s32[]{:S(2)}) async-start(s8[7340032]{0:T(1024)(128)(4,1)} %bitcast.33), calls=%async_computation.6 | async-start | bytes 8388608
  229.0 11.9 %slice-start.1 = ((s8[7340032]{0:T(1024)(128)(4,1)}), s8[3145728]{0:T(1024)(128)(4,1)S(1)}, s32[]{:S(2)}) async-start(s8[7340032]{0:T(1024)(128)(4,1)} %bitcast.33), calls=%async_computation.7 | async-start | bytes 6291456
  251.6 184.1 %copy-start.1 = (bf16[128,3584]{1,0:T(8,128)(2,1)S(1)}, bf16[128,3584]{1,0:T(8,128)(2,1)}, u32[]{:S(2)}) copy-start(bf16[128,3584]{1,0:T(8,128)(2,1)} %param.8) | copy-start | bytes 2752516
Sparse Core Ops, SparseCore 0:
  10.0 101.4 all-gather.2
  114.2 101.1 all-gather.4
  269.5 159.7 reduce-scatter.1
where the time goes:
time: 443 us; the launch traced here: 442 us
  waiting for transfers between devices  338 us (76%)
  matrix products  67.4 us (15%)
  blocking collectives  15.3 us (3%)
  between operations  13.2 us (3%)
  local copies, waits for them, and re-layouts  7.81 us (2%)
    reduce_scatter x1, waiting for transfers between devices, body(): mine = lax.psum_scatter(back, 'ep', scatter_dimension=0, tiled=True)  160 us
    all_gather x1, waiting for transfers between devices, body(): in_rows = lax.all_gather(mine_in, 'ep', axis=0, tiled=True)  90.3 us
    all_gather x1, waiting for transfers between devices, body(): grad_rows = lax.all_gather(mine_grad, 'ep', axis=0, tiled=True)  87.5 us
    dot_general x1, matrix products, body(): lax.dot_general(up_grad, up_mat, nt, preferred_element_type=jnp.float32)  17.7 us
    dot_general x1, matrix products, body(): gate_pre = jnp.dot(in_rows, gate_mat, preferred_element_type=jnp.float32)  13.6 us
    dot_general x1, matrix products, body(): lax.dot_general(grad_rows, down_mat, nt, preferred_element_type=jnp.float32)  13.6 us
    dot_general x1, matrix products, body(): up_pre = jnp.dot(in_rows, up_mat, preferred_element_type=jnp.float32)  11.8 us
    dot_general x1, matrix products, body(): lax.dot_general(gate_grad, gate_mat, nt, preferred_element_type=jnp.float32)  10.7 us
  transfers between devices with their start and end apart: 3, of which 3 were waited for; matrix products, arithmetic and copies ran while one was open for 4% of the time, Pallas kernels for 0%

commit v1 on v0

--- a/solution.py
+++ b/solution.py
@@ -20,8 +20,11 @@
         jnp.where(ids[None, :, :] == names[:, None, None], probs[None, :, :], 0.0), axis=2
     )
     weight = lax.all_to_all(table, "ep", split_axis=0, concat_axis=0, tiled=True).reshape(-1)
-    in_rows = lax.all_gather(mine_in, "ep", axis=0, tiled=True)
-    grad_rows = lax.all_gather(mine_grad, "ep", axis=0, tiled=True)
+    in_rows, grad_rows = jnp.split(
+        lax.all_gather(jnp.concatenate([mine_in, mine_grad], axis=1), "ep", axis=0, tiled=True),
+        [mine_in.shape[1]],
+        axis=1,
+    )
     gate_mat, up_mat, down_mat = (gate_proj[0], up_proj[0], down_proj[0])
     nt = (((1,), (1,)), ((), ()))
     gate_pre = jnp.dot(in_rows, gate_mat, preferred_element_type=jnp.float32)

time: 443 us -> 421 us (0.950)
  waiting for transfers between devices: 338 us -> 318 us
    all_gather x2 -> x1, waiting for transfers between devices: 178 us -> 158 us  [body(): lax.all_gather(jnp.concatenate([mine_in, mine_grad], axis=1), 'ep', axis=...]
  transfers between devices with their start and end apart: 3 -> 2, of which waited for: 3 -> 2; matrix products, arithmetic and copies ran while one was open for 4% -> 1% of each run, Pallas kernels for 0% -> 0%
where the time goes in v1:
time: 421 us; the launch traced here: 420 us
  waiting for transfers between devices  318 us (76%)
  matrix products  67.3 us (16%)
  blocking collectives  15.3 us (4%)
  between operations  13.5 us (3%)
  local copies, waits for them, and re-layouts  4.47 us (1%)
    reduce_scatter x1, waiting for transfers between devices, body(): mine = lax.psum_scatter(back, 'ep', scatter_dimension=0, tiled=True)  160 us
    all_gather x1, waiting for transfers between devices, body(): lax.all_gather(jnp.concatenate([mine_in, mine_grad], axis=1), 'ep', axis=...  158 us
    dot_general x1, matrix products, body(): lax.dot_general(up_grad, up_mat, nt, preferred_element_type=jnp.float32)  17.7 us
    dot_general x1, matrix products, body(): lax.dot_general(gate_grad, gate_mat, nt, preferred_element_type=jnp.float32)  13.7 us
    dot_general x1, matrix products, body(): lax.dot_general(grad_rows, down_mat, nt, preferred_element_type=jnp.float32)  12.9 us
    dot_general x1, matrix products, body(): up_pre = jnp.dot(in_rows, up_mat, preferred_element_type=jnp.float32)  11.7 us
    dot_general x1, matrix products, body(): gate_pre = jnp.dot(in_rows, gate_mat, preferred_element_type=jnp.float32)  11.3 us
    all_to_all x1, blocking collectives, body(): lax.all_to_all(table, 'ep', split_axis=0, concat_axis=0, tiled=True)  10.6 us
  transfers between devices with their start and end apart: 2, of which 2 were waited for; matrix products, arithmetic and copies ran while one was open for 1% of the time, Pallas kernels for 0%

profile of v1, /device:TPU:11, one launch (start us, length us, event | category | flops | bytes accessed | tf_op | source)
XLA Modules:
  0.0 420.5 jit_solution(4722630149337773986)
XLA Ops:
  6.5 0.0 copy-start
  6.5 0.0 all-gather.2.cloned.1.call-start
  6.5 1.2 constant_dynamic-slice_fusion.2
  7.8 1.0 pad_maximum_fusion
  8.8 0.0 all-gather.2.cloned.1.call-update
  8.8 0.0 reduce-scatter.2.cloned.1.call-start
  8.8 0.0 copy-done
  8.8 0.1 constant_dynamic-slice_fusion.1
  8.9 0.8 constant_dynamic-slice_fusion
  9.7 10.6 %all_to_all.28 = f32[16,1,64]{2,1,0:T(1,128)S(1)} all-to-all(f32[16,1,64]{2,1,0:T(1,128)S(1)} %bitcast.29), channel_id=1, replica_groups=mesh['ep'=16,'dp'=2] {'ep'}, dimensions={0} | all-to-all | bytes 8192 | tf_op jit(solution)/shard_map/all_to_all | solution.py:22
  20.3 0.5 broadcast.14
  20.8 0.7 reduce.3
  21.5 0.1 mul.38
  21.6 158.1 %all-gather.2.cloned.1.call-done = bf16[1024,7168]{1,0:T(8,128)(2,1)} async-done(((bf16[64,7168]{1,0:T(8,128)(2,1)}), bf16[1024,7168]{1,0:T(8,128)(2,1)}) %all-gather.2.cloned.1.call-update) | async-done | bytes 14680080 | tf_op jit(solution)/shard_map/all_gather | solution.py:24
  179.7 0.0 copy-start.2
  179.7 11.3 %fusion.4 = f32[1024,1024]{1,0:T(8,128)S(1)} fusion(bf16[1,3584,1024]{2,1,0:T(8,128)(2,1)} %param.11, bf16[1024,7168]{1,0:T(8,128)(2,1)} %all-gather.2.cloned.1.call-done), kind=kOutput, calls=%fused_computation.5 | convolution fusion | flops 7516192768 | bytes 18874368 | tf_op jit(solution)/shard_map/dot_general | solution.py:30
  191.1 0.0 copy-done.2
  191.1 0.0 copy-start.3
  191.1 12.9 %fusion = f32[1024,1024]{1,0:T(8,128)} fusion(bf16[1024,7168]{1,0:T(8,128)(2,1)S(1)} %copy-done.2, bf16[1,1024,3584]{2,1,0:T(8,128)(2,1)} %param.13), kind=kOutput, calls=%fused_computation.1 | convolution fusion | flops 7516192768 | bytes 18874368 | tf_op jit(solution)/shard_map/dot_general | solution.py:32
  204.0 0.0 copy-done.3
  204.0 11.7 %multiply_convert_fusion.2 = bf16[1024,1024]{1,0:T(8,128)(2,1)S(1)} fusion(f32[1024,1024]{1,0:T(8,128)S(1)} %fusion.4, f32[1024,1024]{1,0:T(8,128)} %fusion, bf16[1,3584,1024]{2,1,0:T(8,128)(2,1)} %param.12, bf16[1024,7168]{1,0:T(8,128)(2,1)S(1)} %copy-done.2), kind=kOutput, calls=%fused_computation.14 | convolution fusion | flops 7526678528 | bytes 25165824 | tf_op jit(solution)/shard_map/dot_general | solution.py:31
  215.7 13.7 %fusion.2 = f32[1024,3584]{1,0:T(8,128)} fusion(bf16[1024,1024]{1,0:T(8,128)(2,1)S(1)} %multiply_convert_fusion.2, bf16[1,3584,1024]{2,1,0:T(8,128)(2,1)} %param.11), kind=kOutput, calls=%fused_computation.3 | convolution fusion | flops 7516192768 | bytes 24117248 | tf_op jit(solution)/shard_map/dot_general | solution.py:36
  229.4 0.0 copy-start.1
  229.4 17.7 %multiply_convert_fusion = bf16[1024,3584]{1,0:T(8,128)(2,1)} fusion(f32[1024,3584]{1,0:T(8,128)} %fusion.2, bf16[1,3584,1024]{2,1,0:T(8,128)(2,1)} %param.12, f32[1024]{0:T(1024)S(1)} %mul.38, f32[1024,1024]{1,0:T(8,128)} %fusion, f32[1024,1024]{1,0:T(8,128)} %copy-done.3), kind=kOutput, calls=%fused_computation | convolution fusion | flops 7533494272 | bytes 37752832 | tf_op jit(solution)/shard_map/dot_general | solution.py:37
  247.1 0.0 reduce-scatter.2.cloned.1.call-update
  247.1 160.0 %reduce-scatter.2.cloned.1.call-done = bf16[64,3584]{1,0:T(8,128)(2,1)} async-done(((bf16[1024,3584]{1,0:T(8,128)(2,1)}), bf16[64,3584]{1,0:T(8,128)(2,1)}) %reduce-scatter.2.cloned.1.call-update) | async-done | bytes 458768 | tf_op jit(solution)/shard_map/reduce_scatter | solution.py:39
  407.2 1.0 copy.18
  408.2 4.7 %all_to_all.29 = bf16[64,2,1792]{2,0,1:T(8,128)(2,1)S(1)} all-to-all(bf16[64,2,1792]{2,0,1:T(8,128)(2,1)S(1)} %bitcast.26), channel_id=1, replica_groups=mesh['ep'=16,'dp'=2] {'dp'}, dimensions={1} | all-to-all | bytes 917504 | tf_op jit(solution)/shard_map/all_to_all | solution.py:40
  412.9 0.8 copy.20
  413.6 0.0 copy-done.1
  (1 shorter events, 0.0 us)
Async XLA Ops:
  6.5 2.3 copy-start
  6.5 173.2 %all-gather.2.cloned.1.call-start = ((), (), s32[]{:S(2)}) async-start(), calls=%async_computation.3 | async-start | bytes 15597568 | tf_op jit(solution)/shard_map/all_gather | solution.py:24
  8.8 398.4 %reduce-scatter.2.cloned.1.call-start = ((), (), s32[]{:S(2)}) async-start(), calls=%async_computation.4 | async-start | bytes 7798784 | tf_op jit(solution)/shard_map/reduce_scatter | solution.py:39
  179.7 11.3 %copy-start.2 = (bf16[1024,7168]{1,0:T(8,128)(2,1)S(1)}, bf16[1024,7168]{1,0:T(8,128)(2,1)}, u32[]{:S(2)}) copy-start(bf16[1024,7168]{1,0:T(8,128)(2,1)} %all-gather.2.cloned.1.call-done) | copy-start | bytes 44040196
  191.1 13.0 %copy-start.3 = (f32[1024,1024]{1,0:T(8,128)}, f32[1024,1024]{1,0:T(8,128)S(1)}, u32[]{:S(2)}) copy-start(f32[1024,1024]{1,0:T(8,128)S(1)} %fusion.4) | copy-start | bytes 12582916
  229.4 184.2 %copy-start.1 = (s32[128,8]{0,1:T(8,128)S(1)}, s32[128,8]{0,1:T(8,128)}, u32[]{:S(2)}) copy-start(s32[128,8]{0,1:T(8,128)} %param.9) | copy-start | bytes 12292
Sparse Core Ops, SparseCore 0:
  10.1 169.5 all-gather.1
  247.2 159.8 reduce-scatter.1
